TPU v7x, 32 devices: a whole 2x2x4 slice. The times are simulated.
32 devices in a mesh: node: 4 (over x, core), local: 8 (over z, y).
Axes of the slice: x: 2, y: 2, z: 4, core: 2. Of those that a mesh axis runs over, the one named last changes fastest.
Arguments:
- tokens: bfloat16 [2048, 7168], P(('node', 'local')), may hold values from -6 to 6
- routes: int32 [2048, 2], P(('node', 'local')), may hold values from 0 to 7, as said below
- scores: float32 [2048, 2], P(('node', 'local')), may hold values from 0.1 to 1
- gate_proj: bfloat16 [32, 7168, 512], P(('node', 'local')), may hold values from -0.0625 to 0.0625
- up_proj: bfloat16 [32, 7168, 512], P(('node', 'local')), may hold values from -0.0625 to 0.0625
- down_proj: bfloat16 [32, 512, 7168], P(('node', 'local')), may hold values from -0.125 to 0.125
Outputs:
- combined: bfloat16 [2048, 7168], P(('node', 'local'))
Inputs may be any that keep to these rules, and one draw needn't show every extreme that they name: `routes`: each row names 2 different experts. The rows of one device name each expert at most 20 times, and in every draw one expert is named by exactly 20 rows of every device.
All inputs are finite; a program needn't handle non-finite values.
Results may differ from a plain program's by a relative error of at most 0.0085.
Values may be sent and summed in bfloat16 or wider, within the bound.
A program may use at most 192 MiB of HBM per device.

v0:
```python
import functools

import jax
import jax.numpy as jnp
from jax import lax
from jax.experimental import pallas as pl
from jax.experimental.pallas import tpu as pltpu
from jax.sharding import PartitionSpec as P

SHARDS = 4
SCALE = 2.827
FOLD = 4
MESH = pl.DeviceIdType.MESH


def place(groups):
    node = lax.axis_index("node")
    local = lax.axis_index("local")
    mine = node * groups + local // SHARDS
    block = local % SHARDS
    near = block + 1 - 2 * (block % 2)
    far = (block + 2) % SHARDS
    corner = (near + 2) % SHARDS

    def device(expert, which):
        return (expert // groups, (expert % groups) * SHARDS + which)

    return mine, block, near, far, corner, device


def greet(mine, block, near, far, device, experts):
    barrier = pltpu.get_barrier_semaphore()
    targets = [device((mine + r) % experts, block) for r in range(1, experts)]
    targets += [device(mine, near), device(mine, far)]
    for target in targets:
        pl.semaphore_signal(barrier, inc=1, device_id=target, device_id_type=MESH)
    pl.semaphore_wait(barrier, len(targets))


def over_far(r, every):
    return every > 0 and r % every == 0


def rounds(experts, groups):
    same = [r for r in range(experts) if r % groups == 0]
    return same + [r for r in range(experts) if r % groups]


DISPATCH_FAR = 4
COMBINE_FAR = 0
AHEAD = 4
LAG = 2


class Transfer:
    def __init__(self, src, dst, send, recv, slot, target):
        self.copies = [
            pltpu.make_async_remote_copy(
                src_ref=piece,
                dst_ref=landing,
                send_sem=send.at[slot + (k,)],
                recv_sem=recv.at[slot + (k,)],
                device_id=target,
                device_id_type=MESH,
            )
            for k, (piece, landing) in enumerate(zip(src, dst))
        ]

    def start(self):
        for copy in self.copies:
            copy.start()

    def wait_recv(self):
        for copy in self.copies:
            copy.wait_recv()

    def wait_send(self):
        for copy in self.copies:
            copy.wait_send()


def at(refs, *index):
    return [ref.at[index] for ref in refs]


def dispatch_kernel(experts, groups, pieces, *refs):
    bucket, out = refs[:pieces], refs[pieces : 2 * pieces]
    own_sem, a_send, a_recv, b_send, b_recv, c_send, c_recv = refs[2 * pieces :]
    mine, block, near, far, corner, device = place(groups)
    greet(mine, block, near, far, device, experts)

    order = rounds(experts, groups)
    spread, to_near, to_far, relay = {}, {}, {}, {}
    for r in reversed(order[1:]):
        peer = (mine + r) % experts
        spread[r] = Transfer(at(bucket, peer), at(out, block, mine), a_send, a_recv, (r,), device(peer, block))
        spread[r].start()
    own = [
        pltpu.make_async_copy(src, dst, own_sem.at[k])
        for k, (src, dst) in enumerate(zip(at(bucket, mine), at(out, block, mine)))
    ]
    for copy in own:
        copy.start()

    def forward(r):
        source = (mine + experts - r) % experts
        if over_far(r, DISPATCH_FAR):
            to_near[r].wait_recv()
            moved = at(out, near, source)
            relay[r] = Transfer(moved, moved, c_send, c_recv, (r,), device(mine, far))
        else:
            to_far[r].wait_recv()
            moved = at(out, far, source)
            relay[r] = Transfer(moved, moved, c_send, c_recv, (r,), device(mine, near))
        relay[r].start()

    for step, r in enumerate(order):
        source = (mine + experts - r) % experts
        dst = at(out, block, source)
        if r == 0:
            src = at(bucket, mine)
        else:
            spread[r].wait_recv()
            src = dst
        to_near[r] = Transfer(src, dst, b_send, b_recv, (0, r), device(mine, near))
        to_far[r] = Transfer(src, dst, b_send, b_recv, (1, r), device(mine, far))
        to_near[r].start()
        to_far[r].start()
        if step >= LAG:
            forward(order[step - LAG])
    for r in order[experts - LAG :]:
        forward(r)
    for r in order:
        if over_far(r, DISPATCH_FAR):
            to_far[r].wait_recv()
        else:
            to_near[r].wait_recv()
        relay[r].wait_recv()
    for r in order:
        if r:
            spread[r].wait_send()
        to_near[r].wait_send()
        to_far[r].wait_send()
        relay[r].wait_send()
    for copy in own:
        copy.wait()


def combine_kernel(experts, groups, pieces, *refs):
    part, ret, held, total, back = [refs[k * pieces : (k + 1) * pieces] for k in range(5)]
    a_send, a_recv, b_send, b_recv, c_send, c_recv = refs[5 * pieces :]
    mine, block, near, far, corner, device = place(groups)
    greet(mine, block, near, far, device, experts)

    def add(dst, *terms):
        for k in range(pieces):
            value = terms[0][k][...].astype(jnp.float32)
            for term in terms[1:]:
                value = value + term[k][...].astype(jnp.float32)
            dst[k][...] = value.astype(dst[k].dtype)

    order = rounds(experts, groups)[::-1]
    relay, to_near, to_far, home = {}, {}, {}, {}

    def open_round(r):
        source = (mine + experts - r) % experts
        target = far if over_far(r, COMBINE_FAR) else near
        relay[r] = Transfer(at(part, corner, source), at(held, 2, r), c_send, c_recv, (r,), device(mine, target))
        relay[r].start()
        if over_far(r, COMBINE_FAR):
            to_far[r] = Transfer(at(part, far, source), at(held, 1, r), b_send, b_recv, (1, r), device(mine, far))
            to_far[r].start()
        else:
            to_near[r] = Transfer(at(part, near, source), at(held, 0, r), b_send, b_recv, (0, r), device(mine, near))
            to_near[r].start()

    def send_home(r):
        source = (mine + experts - r) % experts
        to_near[r].wait_recv()
        to_far[r].wait_recv()
        terms = at(part, block, source), at(held, 0, r), at(held, 1, r)
        if r == 0:
            add(at(ret, mine), *terms)
        else:
            add(at(back, r), *terms)
            home[r] = Transfer(at(back, r), at(ret, mine), a_send, a_recv, (r,), device(source, block))
            home[r].start()

    for r in order[:AHEAD]:
        open_round(r)
    for step, r in enumerate(order):
        source = (mine + experts - r) % experts
        relay[r].wait_recv()
        if over_far(r, COMBINE_FAR):
            add(at(total, r), at(part, near, source), at(held, 2, r))
            to_near[r] = Transfer(at(total, r), at(held, 0, r), b_send, b_recv, (0, r), device(mine, near))
            to_near[r].start()
        else:
            add(at(total, r), at(part, far, source), at(held, 2, r))
            to_far[r] = Transfer(at(total, r), at(held, 1, r), b_send, b_recv, (1, r), device(mine, far))
            to_far[r].start()
        if step + AHEAD < experts:
            open_round(order[step + AHEAD])
        if step >= LAG:
            send_home(order[step - LAG])
    for r in order[experts - LAG :]:
        send_home(r)
    for r in order:
        if r:
            home[r].wait_recv()
            home[r].wait_send()
        relay[r].wait_send()
        to_near[r].wait_send()
        to_far[r].wait_send()


def sems(experts, pieces):
    dma = pltpu.SemaphoreType.DMA
    one, two = dma((experts, pieces)), dma((2, experts, pieces))
    return [one, one, two, two, one, one]


def dispatch(bucket, groups):
    experts, pieces = bucket[0].shape[0], len(bucket)
    return pl.pallas_call(
        functools.partial(dispatch_kernel, experts, groups, pieces),
        out_shape=[jax.ShapeDtypeStruct((SHARDS,) + piece.shape, piece.dtype) for piece in bucket],
        in_specs=[pl.BlockSpec(memory_space=pltpu.VMEM)] * pieces,
        out_specs=[pl.BlockSpec(memory_space=pl.ANY)] * pieces,
        scratch_shapes=[pltpu.SemaphoreType.DMA((pieces,))] + sems(experts, pieces),
        compiler_params=pltpu.CompilerParams(collective_id=0, has_side_effects=True),
        name="dispatch",
    )(*bucket)


def combine(part, groups):
    experts, pieces = part[0].shape[1], len(part)
    blocks = [(piece.shape[1:], piece.dtype) for piece in part]
    return pl.pallas_call(
        functools.partial(combine_kernel, experts, groups, pieces),
        out_shape=[jax.ShapeDtypeStruct(shape, kind) for shape, kind in blocks],
        in_specs=[pl.BlockSpec(memory_space=pltpu.VMEM)] * pieces,
        out_specs=[pl.BlockSpec(memory_space=pltpu.VMEM)] * pieces,
        scratch_shapes=[pltpu.VMEM((3,) + shape, kind) for shape, kind in blocks]
        + [pltpu.VMEM(shape, kind) for shape, kind in blocks] * 2
        + sems(experts, pieces),
        compiler_params=pltpu.CompilerParams(
            collective_id=1, has_side_effects=True, vmem_limit_bytes=60 * 2**20
        ),
        name="combine",
    )(*part)


def dot(left, right):
    return jnp.dot(left, right, preferred_element_type=jnp.float32)


def activate(gate_act, up_act):
    return (jax.nn.silu(gate_act) * up_act).astype(jnp.bfloat16)


def expert_block(rows, w_gate, w_up, w_down):
    hidden = activate(dot(rows, w_gate), dot(rows, w_up))
    return dot(hidden, w_down).astype(jnp.bfloat16)


def folded_block(rows, w_gate, w_up, w_down):
    half = rows.shape[1]

    def project(weight):
        left = dot(rows, weight[:half]).reshape(-1, 2, FOLD, weight.shape[1])
        right = dot(rows, weight[half:]).reshape(-1, 2, FOLD, weight.shape[1])
        return left[:, 0] + right[:, 1]

    hidden = activate(project(w_gate), project(w_up))
    twice = jnp.concatenate([hidden, hidden], axis=1).reshape(rows.shape[0], -1)
    upper = jnp.arange(rows.shape[0])[:, None] % (2 * FOLD) < FOLD
    return jnp.where(upper, dot(twice, w_down[:, :half]), dot(twice, w_down[:, half:])).astype(jnp.bfloat16)


def per_device(tokens, routes, scores, gate_proj, up_proj, down_proj):
    node_count = lax.axis_size("node")
    local_count = lax.axis_size("local")
    token_count, model_width = tokens.shape
    top_count = routes.shape[1]
    groups = local_count // SHARDS
    experts = node_count * groups
    per_expert = max(
        2, token_count * top_count // experts + token_count * top_count // (4 * experts)
    )
    tile = 2 * FOLD
    half = model_width // 2
    full = per_expert // tile * tile
    folds = full > 0 and 0 < per_expert - full <= FOLD
    if not folds:
        full = (per_expert + tile - 1) // tile * tile
    cap = full + FOLD if folds else full
    weights = (SCALE * scores / jnp.sum(scores, axis=1, keepdims=True)).astype(jnp.bfloat16)
    labels = jnp.arange(experts, dtype=jnp.int32)
    matches = routes[:, :, None] == labels[None, None, :]
    routed = jnp.any(matches, axis=1)
    dense_weight = jnp.sum(jnp.where(matches, weights.astype(jnp.float32)[:, :, None], 0.0), axis=1)
    position = jnp.cumsum(routed.astype(jnp.int32), axis=0) - 1
    slot_ids = jnp.arange(cap, dtype=jnp.int32)
    pick = routed.T[:, None, :] & (position.T[:, None, :] == slot_ids[None, :, None])
    slot_pick = pick.astype(jnp.bfloat16)
    slot_weight = jnp.where(pick, dense_weight.T[:, None, :], 0.0).astype(jnp.bfloat16)

    def flat(slots):
        return slots.reshape(-1, slots.shape[-1])

    def halves(slots):
        none = jnp.zeros_like(slots)
        return flat(jnp.concatenate([slots, none], axis=1)), flat(jnp.concatenate([none, slots], axis=1))

    bucket = [dot(flat(slot_pick[:, :full]), tokens).astype(jnp.bfloat16).reshape(experts, full, model_width)]
    if folds:
        upper, lower = halves(slot_pick[:, full:])
        folded = (dot(upper, tokens[:, :half]) + dot(lower, tokens[:, half:])).astype(jnp.bfloat16)
        bucket.append(folded.reshape(experts, tile, half))
    gathered = dispatch(bucket, groups)
    blocks = expert_block, folded_block
    part = [
        blocks[k](flat(piece), gate_proj[0], up_proj[0], down_proj[0]).reshape(piece.shape)
        for k, piece in enumerate(gathered)
    ]
    returned = combine(part, groups)
    combined = dot(flat(slot_weight[:, :full]).T, flat(returned[0]))
    if folds:
        upper, lower = halves(slot_weight[:, full:])
        rows = flat(returned[1])
        combined = combined + jnp.concatenate([dot(upper.T, rows), dot(lower.T, rows)], axis=1)
    return combined.astype(jnp.bfloat16)


def solution(mesh):
    return jax.shard_map(
        per_device,
        mesh=mesh,
        in_specs=(
            P(("node", "local"), None),
            P(("node", "local"), None),
            P(("node", "local"), None),
            P(("node", "local"), None, None),
            P(("node", "local"), None, None),
            P(("node", "local"), None, None),
        ),
        out_specs=P(("node", "local"), None),
        check_vma=False,
    )
```

profile of v0, /device:TPU:0, one launch (start us, length us, event | category | flops | bytes accessed | tf_op | source)
XLA Modules:
  0.0 269.0 jit_solution(290016330168002320)
XLA Ops:
  0.0 0.0 copy-start
  0.0 0.8 fusion.63
  0.8 0.1 copy.24
  0.9 0.1 reduce_window_sum.11
  1.0 0.1 copy.25
  1.1 1.3 fusion.49
  2.4 2.1 fusion.8.refs_1_
  4.4 0.0 copy-done
  4.4 1.9 convolution_convert_fusion.1
  6.3 0.0 slice-start
  6.3 119.8 %dispatch.1 = (bf16[4,8,16,7168]{3,2,1,0:T(8,128)(2,1)}, bf16[4,8,8,3584]{3,2,1,0:T(8,128)(2,1)}) custom-call(bf16[8,16,7168]{2,1,0:T(8,128)(2,1)} %bitcast.107, bf16[8,8,3584]{2,1,0:T(8,128)(2,1)} %fusion.8.refs_1_), custom_call_target="tpu_custom_call" | custom-call | tf_op jit(solution)/shard_map/dispatch/pallas_call | solution.py:225
  126.1 0.0 slice-start.2
  126.2 2.2 copy.35
  128.3 0.0 slice-start.1
  128.4 0.0 slice-start.3
  128.4 2.8 %fusion.16 = f32[32,1,4,512]{3,0,2,1:T(8,128)S(1)} fusion(bf16[32,2,4,3584]{3,0,2,1:T(8,128)(2,1)S(1)} %bitcast.108, bf16[1,7168,512]{2,1,0:T(8,128)(2,1)} %param.9), kind=kOutput, calls=%fused_computation.23 | convolution fusion | flops 469762048 | bytes 5767168 | tf_op jit(solution)/shard_map/slice | solution.py:273
  131.2 0.0 slice-done
  131.2 0.6 slice-done.1
  131.8 0.6 fusion.33
  132.4 0.0 slice-done.2
  132.4 0.2 slice-done.3
  132.7 0.0 slice-start.4
  132.7 0.6 fusion.12
  133.3 0.0 slice-start.5
  133.3 0.7 fusion.45
  134.0 0.8 slice-done.4
  134.9 1.1 slice-done.5
  136.0 0.0 slice-start.6
  136.0 1.2 fusion.10
  137.2 0.0 slice-start.7
  137.2 2.6 fusion.6
  139.8 0.0 slice-done.6
  139.8 0.0 slice-done.7
  139.8 4.0 %fusion.4 = f32[512,512]{1,0:T(8,128)S(1)} fusion(bf16[512,7168]{1,0:T(8,128)(2,1)S(1)} %bitcast.127, bf16[1,7168,512]{2,1,0:T(8,128)(2,1)S(1)} %bitcast.118), kind=kOutput, calls=%fused_computation.7 | convolution fusion | flops 3758096384 | bytes 15728640 | tf_op jit(solution)/shard_map/dot_general | solution.py:255
  143.8 4.0 %fusion.27 = bf16[512,512]{1,0:T(8,128)(2,1)S(1)} fusion(bf16[512,7168]{1,0:T(8,128)(2,1)S(1)} %bitcast.128, bf16[1,7168,512]{2,1,0:T(8,128)(2,1)S(1)} %bitcast.120, f32[512,512]{1,0:T(8,128)S(1)} %fusion.4), kind=kOutput, calls=%fused_computation.32 | convolution fusion | flops 3759669248 | bytes 16252928 | tf_op jit(solution)/shard_map/dot_general | solution.py:255
  147.9 6.2 %convolution_convert_fusion = bf16[512,7168]{1,0:T(8,128)(2,1)} fusion(bf16[512,512]{1,0:T(8,128)(2,1)S(1)} %fusion.27, bf16[1,512,7168]{2,1,0:T(8,128)(2,1)S(1)} %bitcast.122), kind=kOutput, calls=%fused_computation | convolution fusion | flops 3761766400 | bytes 15204352 | tf_op jit(solution)/shard_map/dot_general | solution.py:255
  154.1 0.0 copy-start.2
  154.1 0.0 copy-start.3
  154.1 110.6 %combine.1 = (bf16[8,16,7168]{2,1,0:T(8,128)(2,1)}, bf16[8,8,3584]{2,1,0:T(8,128)(2,1)}) custom-call(bf16[4,8,16,7168]{3,2,1,0:T(8,128)(2,1)} %bitcast.106, bf16[4,8,8,3584]{3,2,1,0:T(8,128)(2,1)} %bitcast.112), custom_call_target="tpu_custom_call" | custom-call | tf_op jit(solution)/shard_map/combine/pallas_call | solution.py:239
  264.6 0.0 copy-start.1
  264.6 0.0 copy-done.2
  264.7 0.0 copy-done.3
  264.8 1.5 convolution_bitcast_fusion.2
  266.2 1.4 convolution_bitcast_fusion.1
  267.6 0.0 copy-done.1
  267.6 1.4 fusion.1
  (16 shorter events, 0.2 us)
Async XLA Ops:
  0.0 4.4 %copy-start = (bf16[64,7168]{1,0:T(8,128)(2,1)S(1)}, bf16[64,7168]{1,0:T(8,128)(2,1)}, u32[]{:S(2)}) copy-start(bf16[64,7168]{1,0:T(8,128)(2,1)} %param.6) | copy-start | bytes 2752516
  6.3 124.9 %slice-start = ((s8[7340032]{0:T(1024)(128)(4,1)}), s8[3145728]{0:T(1024)(128)(4,1)S(1)}, s32[]{:S(2)}) async-start(s8[7340032]{0:T(1024)(128)(4,1)} %bitcast.117), calls=%async_computation | async-start | bytes 6291456
  126.1 6.3 %slice-start.2 = ((s8[7340032]{0:T(1024)(128)(4,1)}), s8[4194304]{0:T(1024)(128)(4,1)S(1)}, s32[]{:S(2)}) async-start(s8[7340032]{0:T(1024)(128)(4,1)} %bitcast.119), calls=%async_computation.2 | async-start | bytes 8388608
  128.3 3.4 %slice-start.1 = ((s8[7340032]{0:T(1024)(128)(4,1)}), s8[4194304]{0:T(1024)(128)(4,1)S(1)}, s32[]{:S(2)}) async-start(s8[7340032]{0:T(1024)(128)(4,1)} %bitcast.117), calls=%async_computation.1 | async-start | bytes 8388608
  128.4 4.3 %slice-start.3 = ((s8[7340032]{0:T(1024)(128)(4,1)}), s8[3145728]{0:T(1024)(128)(4,1)S(1)}, s32[]{:S(2)}) async-start(s8[7340032]{0:T(1024)(128)(4,1)} %bitcast.119), calls=%async_computation.3 | async-start | bytes 6291456
  132.7 2.2 slice-start.4
  133.3 2.7 slice-start.5
  136.0 3.8 %slice-start.6 = ((s8[7340032]{0:T(1024)(128)(4,1)}), s8[4194304]{0:T(1024)(128)(4,1)S(1)}, s32[]{:S(2)}) async-start(s8[7340032]{0:T(1024)(128)(4,1)} %bitcast.125), calls=%async_computation.6 | async-start | bytes 8388608
  137.2 2.6 slice-start.7
  154.1 110.6 %copy-start.2 = (f32[64,2]{0,1:T(2,128)S(1)}, f32[64,2]{0,1:T(2,128)}, u32[]{:S(2)}) copy-start(f32[64,2]{0,1:T(2,128)} %param.8) | copy-start | bytes 1540
  154.1 110.6 %copy-start.3 = (s32[64,2]{0,1:T(2,128)S(1)}, s32[64,2]{0,1:T(2,128)}, u32[]{:S(2)}) copy-start(s32[64,2]{0,1:T(2,128)} %param.7) | copy-start | bytes 1540
  264.6 2.9 %copy-start.1 = (bf16[8,16,7168]{2,1,0:T(8,128)(2,1)S(1)}, bf16[8,16,7168]{2,1,0:T(8,128)(2,1)}, u32[]{:S(2)}) copy-start(bf16[8,16,7168]{2,1,0:T(8,128)(2,1)} %get-tuple-element.11) | copy-start | bytes 5505028
where the time goes:
time: 271 us; the launch traced here: 269 us
  Pallas kernels  230 us (85%)
  matrix products  32.2 us (12%)
  local copies, waits for them, and re-layouts  5.17 us (2%)
    pallas_call x1, Pallas kernels, dispatch(): pl.pallas_call(functools.partial(dispatch_kernel, experts, groups, pieces...  120 us
    pallas_call x1, Pallas kernels, combine(): pl.pallas_call(functools.partial(combine_kernel, experts, groups, pieces)...  111 us
    dot_general x11, matrix products, dot(): return jnp.dot(left, right, preferred_element_type=jnp.float32)  27.5 us

commit v1 on v0

--- a/solution.py
+++ b/solution.py
@@ -278,7 +278,7 @@
     return jnp.where(upper, dot(twice, w_down[:, :half]), dot(twice, w_down[:, half:])).astype(jnp.bfloat16)
 
 
-def per_device(tokens, routes, scores, gate_proj, up_proj, down_proj):
+def bucketed(tokens, routes, scores, gate_proj, up_proj, down_proj):
     node_count = lax.axis_size("node")
     local_count = lax.axis_size("local")
     token_count, model_width = tokens.shape
@@ -333,6 +333,485 @@
     return combined.astype(jnp.bfloat16)
 
 
+CORES = 2
+SQUARES = 4
+PARTS = 2
+DISPATCH_VIA_FAR = (1, 5,)
+COMBINE_VIA_FAR = (0,)
+SCHEDULE = [
+    ("spread", 5), ("spread", 3), ("spread", 1), ("far", 0), ("near", 0), ("near", 4),
+    ("tables", 0), ("spread", 6), ("near", 5), ("near", 1), ("far", 3), ("swap1", 5),
+    ("far", 6), ("near", 3), ("spread", 7), ("far", 1), ("swap0", 5), ("pass_on", 0),
+    ("pass_on", 1), ("swap0", 6), ("pass_on", 3), ("share", 0), ("near", 6), ("far", 7),
+    ("pass_on", 6), ("far", 4), ("share", 3), ("compute", 0), ("spread", 2), ("swap2", 6),
+    ("near", 7), ("swap1", 6), ("compute", 3), ("share", 1), ("swap3", 6), ("swap0", 7),
+    ("pass_on", 7), ("join", 3), ("hop", 3), ("join", 0), ("swap1", 4), ("swap0", 4),
+    ("pass_on", 5), ("compute", 1), ("far", 5), ("share", 7), ("swap1", 7), ("swap3", 7),
+    ("swap2", 4), ("hop", 0), ("join", 1), ("pass_on", 4), ("far", 2), ("near", 2),
+    ("swap2", 7), ("hop", 1), ("compute", 7), ("swap3", 4), ("side", 3), ("middle", 3),
+    ("share", 6), ("swap3", 5), ("swap2", 5), ("join", 7), ("compute", 6), ("share", 4),
+    ("side", 0), ("pass_on", 2), ("share", 5), ("side", 1), ("join", 6), ("middle", 1),
+    ("hop", 6), ("finish", 3), ("share", 2), ("compute", 4), ("hop", 7), ("compute", 2),
+    ("middle", 6), ("join", 4), ("side", 6), ("join", 2), ("middle", 7), ("side", 7),
+    ("compute", 5), ("finish", 6), ("hop", 2), ("join", 5), ("hop", 5), ("middle", 0),
+    ("side", 2), ("middle", 2), ("finish", 7), ("hop", 4), ("middle", 5), ("finish", 2),
+    ("finish", 1), ("side", 5), ("side", 4), ("middle", 4), ("finish", 0), ("finish", 5),
+    ("finish", 4),
+]
+
+
+class Flow:
+    def __init__(self, **spec):
+        self.spec = spec
+        self.started = self.sent = self.landed = False
+
+    def start(self):
+        self.copy = pltpu.make_async_remote_copy(device_id_type=MESH, **self.spec)
+        self.copy.start()
+        self.started = True
+
+    def wait_send(self):
+        if self.started and not self.sent:
+            self.copy.wait_send()
+        self.sent = True
+
+    def wait_recv(self):
+        if self.started and not self.landed:
+            self.copy.wait_recv()
+        self.landed = True
+
+
+def slots_of(token_count, top_count, experts):
+    per_expert = max(2, token_count * top_count // experts + token_count * top_count // (4 * experts))
+    seen = CORES * per_expert
+    return seen, token_count - seen, 2 * seen - token_count
+
+
+def flip(value, by):
+    return 1 - value if by else value
+
+
+def prepare_kernel(groups, private, shared, table_ref, tokens_ref, lists_ref, pick_ref, weight_ref):
+    node = lax.axis_index("node")
+    local = lax.axis_index("local")
+    side, core, half = node // CORES, node % CORES, local // SHARDS
+    count = table_ref.shape[1]
+    listed = count // 2
+    swap = shared // 2
+    first, second = table_ref[0:1, :], table_ref[1:2, :]
+    score_first, score_second = table_ref[2:3, :], table_ref[3:4, :]
+    total = score_first + score_second
+    weight_first = (SCALE * score_first / total).astype(jnp.bfloat16).astype(jnp.float32)
+    weight_second = (SCALE * score_second / total).astype(jnp.bfloat16).astype(jnp.float32)
+
+    def named(expert):
+        name = expert.astype(jnp.float32)
+        return jnp.where(first == name, 1.0, 0.0) + jnp.where(second == name, 1.0, 0.0)
+
+    def weight_row(expert):
+        name = expert.astype(jnp.float32)
+        return jnp.where(first == name, weight_first, 0.0) + jnp.where(second == name, weight_second, 0.0)
+
+    def expert_at(dx, dh, dc):
+        return (flip(side, dx) * CORES + flip(core, dc)) * groups + flip(half, dh)
+
+    row = lax.broadcasted_iota(jnp.int32, (count, count), 0)
+    col = lax.broadcasted_iota(jnp.int32, (count, count), 1)
+    before = jnp.where(row < col, 1.0, 0.0).astype(jnp.bfloat16)
+    slot = row.astype(jnp.float32)
+    picks = []
+    for dh in range(2):
+        on = [jnp.minimum(named(expert_at(dx, dh, 0)) + named(expert_at(dx, dh, 1)), 1.0) for dx in range(2)]
+        both = on[0] * on[1]
+        only = [on[0] - both, on[1] - both]
+        stack = jnp.concatenate([both, only[0], only[1], jnp.zeros((5, count), jnp.float32)], axis=0)
+        rank = dot(stack.astype(jnp.bfloat16), before)
+        both_rank = rank[0:1]
+        both_count = jnp.sum(both, axis=1, keepdims=True)
+        spilled = jnp.maximum(both_count - shared, 0.0)
+        held = jnp.minimum(both_count, float(shared))
+
+        def shared_slot(index):
+            return jnp.where(index < swap, private + index, listed + private + index - swap)
+
+        place = [spilled + rank[1:2], spilled + rank[2:3]]
+        over = [shared_slot(held + place[0] - private), shared_slot(shared - 1 - (place[1] - private))]
+        main = jnp.where(both_rank < shared, shared_slot(both_rank), both_rank - shared)
+        main = jnp.where(both > 0, main, -1.0)
+        for dx in range(2):
+            here = jnp.where(place[dx] < private, dx * listed + place[dx], over[dx])
+            main = jnp.where(only[dx] > 0, here, main)
+        again = jnp.where((both > 0) & (both_rank >= shared), listed + both_rank - shared, -1.0)
+        pick = jnp.where((slot == main) | (slot == again), 1.0, 0.0)
+        picks.append(pick)
+        for dx in range(2):
+            mine = pick[dx * listed : (dx + 1) * listed]
+            other = pick[(1 - dx) * listed + private : (2 - dx) * listed]
+            r = 2 * dh + dx
+            seen = jnp.concatenate(
+                [mine, other, jnp.zeros((128 - listed - swap, count), jnp.float32)], axis=0
+            ).astype(jnp.bfloat16)
+            rows = jnp.concatenate(
+                [weight_row(expert_at(dx, dh, dc)) for dc in range(2)] + [jnp.zeros((6, count), jnp.float32)], axis=0
+            ).astype(jnp.bfloat16)
+            values = lax.dot_general(rows, seen, (((1,), (1,)), ((), ())), preferred_element_type=jnp.float32)
+            for dc in range(2):
+                weight_ref[r, dc] = jnp.broadcast_to(values[dc : dc + 1], (8, 128))
+    pick = jnp.concatenate(picks, axis=0).astype(jnp.bfloat16)
+    pick_ref[...] = pick
+    width = 1024
+
+    def fill(step, carry):
+        columns = pl.ds(pl.multiple_of(step * width, width), width)
+        rows = dot(pick, tokens_ref[:, columns]).astype(jnp.bfloat16)
+        for r in range(SQUARES):
+            lists_ref[r, :, columns] = rows[r * listed : (r + 1) * listed]
+        return carry
+
+    lax.fori_loop(0, tokens_ref.shape[1] // width, fill, 0)
+
+
+def prepare(table, tokens, groups, private, shared):
+    count, model_width = tokens.shape
+    vmem = pl.BlockSpec(memory_space=pltpu.VMEM)
+    return pl.pallas_call(
+        functools.partial(prepare_kernel, groups, private, shared),
+        out_shape=[
+            jax.ShapeDtypeStruct((SQUARES, count // 2, model_width), jnp.bfloat16),
+            jax.ShapeDtypeStruct((2 * count, count), jnp.bfloat16),
+            jax.ShapeDtypeStruct((SQUARES, CORES, 8, 128), jnp.float32),
+        ],
+        in_specs=[vmem, vmem],
+        out_specs=[vmem] * 3,
+        name="prepare",
+    )(table, tokens)
+
+
+def layer_kernel(
+    listed, swap, lists, weight, gate_hbm, up_hbm, down_hbm, ret,
+    gate, up, down, rows_a, rows_b, table, given_a, given_b, extra, held_a, held_b, hidden,
+    load_sem, own_sem, t_send, t_recv, send, recv,
+):
+    node = lax.axis_index("node")
+    local = lax.axis_index("local")
+    side, core = node // CORES, node % CORES
+    half, block = local // SHARDS, local % SHARDS
+    deep, across = block // 2, block % 2
+    part = listed // PARTS
+    rows, given, held = (rows_a, rows_b), (given_a, given_b), (held_a, held_b)
+    lane = [rows[p].shape[2] for p in range(PARTS)]
+
+    def device(r, dc, db):
+        to_block = flip(deep, db // 2) * 2 + flip(across, db % 2)
+        return (flip(side, r % 2) * CORES + flip(core, dc), flip(half, r // 2) * SHARDS + to_block)
+
+    offsets = [(r, dc, db) for r in range(SQUARES) for dc in range(CORES) for db in range(SHARDS)][1:]
+    barrier = pltpu.get_barrier_semaphore()
+    for offset in offsets:
+        pl.semaphore_signal(barrier, inc=1, device_id=device(*offset), device_id_type=MESH)
+
+    loads = [
+        pltpu.make_async_copy(src.at[0], dst, load_sem.at[k])
+        for k, (src, dst) in enumerate(((gate_hbm, gate), (up_hbm, up), (down_hbm, down)))
+    ]
+    own = [
+        pltpu.make_async_copy(
+            lists.at[0, pl.ds(p * part, part)], rows[p].at[0, 0, pl.ds(0, part)], own_sem.at[p]
+        )
+        for p in range(PARTS)
+    ]
+    own.append(pltpu.make_async_copy(weight.at[0, 0], table.at[0, 0, 0], own_sem.at[PARTS]))
+    for copy in own + loads:
+        copy.start()
+    pl.semaphore_wait(barrier, len(offsets))
+    waited = set()
+
+    def once(*names):
+        for name in names:
+            if name not in waited:
+                waited.add(name)
+                (own + loads)[name].wait()
+
+    everything = []
+
+    def flow(kind, q, there, src, dst, target):
+        made = Flow(
+            src_ref=src, dst_ref=dst, send_sem=send.at[kind, q], recv_sem=recv.at[kind, there], device_id=target
+        )
+        everything.append(made)
+        return made
+
+    def piece(ref, r, p):
+        return ref.at[r, pl.ds(p * part, part)]
+
+    def entry(q, db):
+        return rows[q // SQUARES].at[q % SQUARES, 0, pl.ds(db * part, part)]
+
+    def last_rows(r, db):
+        return rows[1].at[r, 0, pl.ds(db * part + part - swap, swap)]
+
+    def other_rows(r, db):
+        return rows[1].at[r, 0, pl.ds(SHARDS * part + db * swap, swap)]
+
+    def other(q):
+        return q + 1 - 2 * (q % 2)
+
+    spread, near, far, relay, shared = {}, {}, {}, {}, {}
+    out, hop, side_sum, far_sum, home, swapped, patch = {}, {}, {}, {}, {}, {}, {}
+    y_way, z_way = device(0, 0, 1), device(0, 0, 2)
+    for q in range(PARTS * SQUARES):
+        p, r = q // SQUARES, q % SQUARES
+        first = entry(q, 0) if r else piece(lists, 0, p)
+        if r:
+            spread[q] = flow(0, q, q, piece(lists, r, p), entry(q, 0), device(r, 0, 0))
+            home[q] = flow(9, q, q, entry(q, 0), piece(ret, r, p), device(r, 0, 0))
+        near[q] = flow(1, q, q, first, entry(q, 1), y_way)
+        far[q] = flow(2, q, q, first, entry(q, 2), z_way)
+        if q in DISPATCH_VIA_FAR:
+            relay[q] = flow(3, q, q, entry(q, 1), entry(q, 3), z_way)
+        else:
+            relay[q] = flow(3, q, q, entry(q, 2), entry(q, 3), y_way)
+        shared[q] = flow(4, q, q, rows[p].at[r, 0], rows[p].at[r, 1], device(0, 1, 0))
+        out[q] = flow(5, q, q, rows[p].at[r, 1], given[p].at[r], device(0, 1, 0))
+        early, late = (2, 1) if q in COMBINE_VIA_FAR else (1, 2)
+        early_way, late_way = device(0, 0, early), device(0, 0, late)
+        hop[q] = flow(6, q, q, entry(q, 3), held[p].at[2, r], early_way)
+        side_sum[q] = flow(7, q, q, entry(q, early), held[p].at[0, r], early_way)
+        far_sum[q] = flow(8, q, q, held[p].at[2, r], held[p].at[1, r], late_way)
+        if p:
+            for db in range(SHARDS):
+                swapped[q, db] = flow(
+                    10 + db, q, other(q), last_rows(r, db), other_rows(other(r), db), device(1, 0, 0)
+                )
+                patch[q, db] = flow(
+                    14 + db,
+                    q,
+                    other(q),
+                    other_rows(r, db),
+                    extra.at[other(r), pl.ds(db * swap, swap)],
+                    device(1, 0, 0),
+                )
+    tables = [
+        Flow(
+            src_ref=weight.at[r, dc],
+            dst_ref=table.at[r, dc, db],
+            send_sem=t_send.at[r, dc, db],
+            recv_sem=t_recv.at[r, dc, db],
+            device_id=device(r, dc, db),
+        )
+        for r, dc, db in offsets
+    ]
+    everything.extend(tables)
+
+    def add_into(target, *terms):
+        value = target[...].astype(jnp.float32)
+        for term in terms:
+            value = value + term[...].astype(jnp.float32)
+        target[...] = value.astype(target.dtype)
+
+    def landed(q, db):
+        if db == 0:
+            if q % SQUARES:
+                spread[q].wait_recv()
+            else:
+                once(q // SQUARES)
+        else:
+            (None, near, far, relay)[db][q].wait_recv()
+
+    def send_near(q):
+        if q % SQUARES:
+            spread[q].wait_recv()
+        near[q].start()
+
+    def send_far(q):
+        if q % SQUARES:
+            spread[q].wait_recv()
+        far[q].start()
+
+    def pass_on(q):
+        landed(q, 1 if q in DISPATCH_VIA_FAR else 2)
+        relay[q].start()
+
+    def swap_rows(q, db):
+        landed(q, db)
+        swapped[q, db].start()
+
+    def share(q):
+        for db in range(SHARDS):
+            landed(q, db)
+        if q >= SQUARES:
+            for db in range(SHARDS):
+                swapped[other(q), db].wait_recv()
+        shared[q].start()
+
+    def column(q):
+        p, r = q // SQUARES, q % SQUARES
+        spans = [(part, p * part)] + ([(swap, listed)] if p else [])
+        values = []
+        for dc in range(CORES):
+            for size, shift in spans:
+                lanes = lax.broadcasted_iota(jnp.int32, (size, 128), 1)
+                spots = lax.broadcasted_iota(jnp.int32, (size, 128), 0) + shift
+                for db in range(SHARDS):
+                    chosen = jnp.where(lanes == spots, table[r, dc, db, 0:1, :], 0.0)
+                    values.append(jnp.sum(chosen, axis=1, keepdims=True))
+        return jnp.concatenate(values, axis=0)
+
+    def compute(q):
+        p, r = q // SQUARES, q % SQUARES
+        once(PARTS, PARTS + 1, PARTS + 2)
+        for copy in tables:
+            copy.wait_recv()
+        shared[q].wait_recv()
+        size = CORES * lane[p]
+        scale = column(q)
+        tile = 256
+
+        def open_up(step, carry):
+            columns = pl.ds(pl.multiple_of(step * tile, tile), tile)
+            left = rows[p][r].reshape(size, down.shape[1])
+            gate_act = dot(left, gate[:, columns])
+            up_act = dot(left, up[:, columns])
+            hidden[:size, columns] = (jax.nn.silu(gate_act) * up_act * scale).astype(jnp.bfloat16)
+            return carry
+
+        lax.fori_loop(0, gate.shape[1] // tile, open_up, 0)
+        once(PARTS + 3)
+        for sent in [near[q], far[q], relay[q], shared[q]] + [swapped[q, db] for db in range(SHARDS) if p]:
+            sent.wait_send()
+        wide = 1024
+
+        def close(step, carry):
+            columns = pl.ds(pl.multiple_of(step * wide, wide), wide)
+            result = dot(hidden[:size], down[:, columns]).astype(jnp.bfloat16)
+            rows[p][r, 0, :, columns] = result[: lane[p]]
+            rows[p][r, 1, :, columns] = result[lane[p] :]
+            return carry
+
+        lax.fori_loop(0, down.shape[1] // wide, close, 0)
+        out[q].start()
+
+    def join(q):
+        p, r = q // SQUARES, q % SQUARES
+        out[q].wait_recv()
+        if p:
+            for db in (3, 1, 2, 0):
+                add_into(other_rows(r, db), given[p].at[r, pl.ds(SHARDS * part + db * swap, swap)])
+                patch[q, db].start()
+        for db in range(SHARDS):
+            add_into(entry(q, db), given[p].at[r, pl.ds(db * part, part)])
+
+    def mended(q, db):
+        if q >= SQUARES:
+            patch[other(q), db].wait_recv()
+            add_into(last_rows(q % SQUARES, db), extra.at[q % SQUARES, pl.ds(db * swap, swap)])
+
+    def send_hop(q):
+        mended(q, 3)
+        hop[q].start()
+
+    def send_side(q):
+        mended(q, 2 if q in COMBINE_VIA_FAR else 1)
+        side_sum[q].start()
+
+    def middle(q):
+        late = 1 if q in COMBINE_VIA_FAR else 2
+        mended(q, late)
+        hop[q].wait_recv()
+        add_into(held[q // SQUARES].at[2, q % SQUARES], entry(q, late))
+        far_sum[q].start()
+
+    def finish(q):
+        p, r = q // SQUARES, q % SQUARES
+        mended(q, 0)
+        side_sum[q].wait_recv()
+        far_sum[q].wait_recv()
+        if r:
+            add_into(entry(q, 0), held[p].at[0, r], held[p].at[1, r])
+            home[q].start()
+        else:
+            value = entry(q, 0)[...].astype(jnp.float32)
+            value = value + held[p][0, r].astype(jnp.float32) + held[p][1, r].astype(jnp.float32)
+            piece(ret, 0, p)[...] = value.astype(ret.dtype)
+
+    steps = dict(
+        spread=lambda q: spread[q].start(), near=send_near, far=send_far, pass_on=pass_on, share=share,
+        compute=compute, join=join, hop=send_hop, side=send_side, middle=middle, finish=finish,
+        tables=lambda q: [copy.start() for copy in tables],
+    )
+    for db in range(SHARDS):
+        steps[f"swap{db}"] = functools.partial(swap_rows, db=db)
+    for name, q in SCHEDULE:
+        steps[name](q)
+    once(*range(PARTS + 4))
+    for made in everything:
+        made.wait_recv()
+        made.wait_send()
+
+
+def layer(lists, weight, gate_proj, up_proj, down_proj, swap):
+    _, listed, model_width = lists.shape
+    hidden_width = gate_proj.shape[2]
+    part = listed // PARTS
+    lanes = (SHARDS * part, SHARDS * (part + swap))
+    dma = pltpu.SemaphoreType.DMA
+    vmem = pl.BlockSpec(memory_space=pltpu.VMEM)
+    hbm = pl.BlockSpec(memory_space=pl.ANY)
+
+    def space(*shape):
+        return pltpu.VMEM(shape, jnp.bfloat16)
+
+    return pl.pallas_call(
+        functools.partial(layer_kernel, listed, swap),
+        out_shape=jax.ShapeDtypeStruct(lists.shape, jnp.bfloat16),
+        in_specs=[vmem, vmem, hbm, hbm, hbm],
+        out_specs=vmem,
+        scratch_shapes=[
+            space(*gate_proj.shape[1:]),
+            space(*up_proj.shape[1:]),
+            space(*down_proj.shape[1:]),
+            space(SQUARES, CORES, lanes[0], model_width),
+            space(SQUARES, CORES, lanes[1], model_width),
+            pltpu.VMEM((SQUARES, CORES, SHARDS, 8, 128), jnp.float32),
+            space(SQUARES, lanes[0], model_width),
+            space(SQUARES, lanes[1], model_width),
+            space(SQUARES, SHARDS * swap, model_width),
+            space(3, SQUARES, part, model_width),
+            space(3, SQUARES, part, model_width),
+            space(CORES * lanes[1], hidden_width),
+            dma((3,)),
+            dma((PARTS + 1,)),
+            dma((SQUARES, CORES, SHARDS)),
+            dma((SQUARES, CORES, SHARDS)),
+            dma((18, PARTS * SQUARES)),
+            dma((18, PARTS * SQUARES)),
+        ],
+        compiler_params=pltpu.CompilerParams(
+            collective_id=2, has_side_effects=True, vmem_limit_bytes=67043328
+        ),
+        name="layer",
+    )(lists, weight, gate_proj, up_proj, down_proj)
+
+
+def per_device(tokens, routes, scores, gate_proj, up_proj, down_proj):
+    node_count = lax.axis_size("node")
+    local_count = lax.axis_size("local")
+    token_count, top_count = routes.shape
+    groups = local_count // SHARDS
+    experts = node_count * groups
+    seen, private, shared = slots_of(token_count, top_count, experts)
+    square = node_count == 2 * CORES and groups == 2 and top_count == 2
+    fits = private > 0 and shared > 0 and private % 8 == 0 and shared % 16 == 0 and token_count % 32 == 0
+    if not (square and fits):
+        return bucketed(tokens, routes, scores, gate_proj, up_proj, down_proj)
+    table = jnp.concatenate([routes.astype(jnp.float32), scores], axis=1).T
+    lists, pick, weight = prepare(table, tokens, groups, private, shared)
+    returned = layer(lists, weight, gate_proj, up_proj, down_proj, shared // 2)
+    flat = returned.reshape(-1, returned.shape[-1])
+    combined = lax.dot_general(pick, flat, (((0,), (0,)), ((), ())), preferred_element_type=jnp.float32)
+    return combined.astype(jnp.bfloat16)
+
+
 def solution(mesh):
     return jax.shard_map(
         per_device,

time: 271 us -> 177 us (0.65)
  Pallas kernels: 230 us -> 172 us
  matrix products: 32.2 us -> 2.88 us
  local copies, waits for them, and re-layouts: 5.17 us -> 0 us
    pallas_call x2, Pallas kernels: 230 us -> 172 us  [the longest x1 168 us: layer(): pl.pallas_call(functools.partial(layer_kernel, listed, swap), out_shape=j...]
    dot_general x11 -> x1, matrix products: 27.5 us -> 2.88 us  [per_device(): lax.dot_general(pick, flat, (((0,), (0,)), ((), ())), preferred_element_t...]
    slice x4 -> x0, matrix products: 4.76 us -> none  [project(): return left[:, 0] + right[:, 1]]
    unnamed x24 -> x0, local copies, waits for them, and re-layouts: 2.83 us -> none
where the time goes in v1:
time: 177 us
  Pallas kernels  172 us (97%)
  matrix products  2.88 us (2%)
  other arithmetic  1.95 us (1%)
    pallas_call x1, Pallas kernels, layer(): pl.pallas_call(functools.partial(layer_kernel, listed, swap), out_shape=j...  168 us
    pallas_call x1, Pallas kernels, prepare(): pl.pallas_call(functools.partial(prepare_kernel, groups, private, shared)...  4.32 us

profile of v1, /device:TPU:0, one launch (start us, length us, event | category | flops | bytes accessed | tf_op | source)
XLA Modules:
  0.0 177.1 jit_solution(12164294214086755406)
XLA Ops:
  0.0 0.7 convert_element_type.6
  0.7 1.3 maximum_bitcast_fusion.table_ref
  2.0 4.3 %prepare.1 = (bf16[4,32,7168]{2,1,0:T(8,128)(2,1)}, bf16[128,64]{1,0:T(8,128)(2,1)}, f32[4,2,8,128]{3,2,1,0:T(8,128)}) custom-call(f32[4,64]{1,0:T(4,128)} %maximum_bitcast_fusion.table_ref, bf16[64,7168]{1,0:T(8,128)(2,1)} %tokens_ref.1), custom_call_target="tpu_custom_call" | custom-call | tf_op jit(solution)/shard_map/prepare/pallas_call | solution.py:477
  6.3 167.9 %layer.1 = bf16[4,32,7168]{2,1,0:T(8,128)(2,1)} custom-call(bf16[4,32,7168]{2,1,0:T(8,128)(2,1)} %get-tuple-element.9.lists, f32[4,2,8,128]{3,2,1,0:T(8,128)} %get-tuple-element.10.weight, bf16[1,7168,512]{2,1,0:T(8,128)(2,1)} %gate_hbm.1, bf16[1,7168,512]{2,1,0:T(8,128)(2,1)} %up_hbm.1, bf16[1,512,7168]{2,1,0:T(8,128)(2,1)} %down_hbm.1), custom_call_target="tpu_custom_call" | custom-call | tf_op jit(solution)/shard_map/layer/pallas_call | solution.py:764
  174.2 2.9 %convolution_convert_fusion = bf16[64,7168]{1,0:T(8,128)(2,1)} fusion(bf16[128,64]{1,0:T(8,128)(2,1)} %get-tuple-element.8, bf16[128,7168]{1,0:T(8,128)(2,1)} %bitcast.5), kind=kOutput, calls=%fused_computation | convolution fusion | flops 117899264 | bytes 2768896 | tf_op jit(solution)/shard_map/dot_general | solution.py:811

commit v2 on v1

--- a/solution.py
+++ b/solution.py
@@ -336,26 +336,27 @@
 CORES = 2
 SQUARES = 4
 PARTS = 2
-DISPATCH_VIA_FAR = (1, 5,)
-COMBINE_VIA_FAR = (0,)
+LATE = 2
+DISPATCH_VIA_FAR = (5,)
+COMBINE_VIA_FAR = (1, 3,)
 SCHEDULE = [
-    ("spread", 5), ("spread", 3), ("spread", 1), ("far", 0), ("near", 0), ("near", 4),
-    ("tables", 0), ("spread", 6), ("near", 5), ("near", 1), ("far", 3), ("swap1", 5),
-    ("far", 6), ("near", 3), ("spread", 7), ("far", 1), ("swap0", 5), ("pass_on", 0),
-    ("pass_on", 1), ("swap0", 6), ("pass_on", 3), ("share", 0), ("near", 6), ("far", 7),
-    ("pass_on", 6), ("far", 4), ("share", 3), ("compute", 0), ("spread", 2), ("swap2", 6),
-    ("near", 7), ("swap1", 6), ("compute", 3), ("share", 1), ("swap3", 6), ("swap0", 7),
-    ("pass_on", 7), ("join", 3), ("hop", 3), ("join", 0), ("swap1", 4), ("swap0", 4),
-    ("pass_on", 5), ("compute", 1), ("far", 5), ("share", 7), ("swap1", 7), ("swap3", 7),
-    ("swap2", 4), ("hop", 0), ("join", 1), ("pass_on", 4), ("far", 2), ("near", 2),
-    ("swap2", 7), ("hop", 1), ("compute", 7), ("swap3", 4), ("side", 3), ("middle", 3),
-    ("share", 6), ("swap3", 5), ("swap2", 5), ("join", 7), ("compute", 6), ("share", 4),
-    ("side", 0), ("pass_on", 2), ("share", 5), ("side", 1), ("join", 6), ("middle", 1),
-    ("hop", 6), ("finish", 3), ("share", 2), ("compute", 4), ("hop", 7), ("compute", 2),
-    ("middle", 6), ("join", 4), ("side", 6), ("join", 2), ("middle", 7), ("side", 7),
-    ("compute", 5), ("finish", 6), ("hop", 2), ("join", 5), ("hop", 5), ("middle", 0),
-    ("side", 2), ("middle", 2), ("finish", 7), ("hop", 4), ("middle", 5), ("finish", 2),
-    ("finish", 1), ("side", 5), ("side", 4), ("middle", 4), ("finish", 0), ("finish", 5),
+    ("spread", 6), ("spread", 5), ("spread", 1), ("tables", 0), ("near", 0), ("near", 4),
+    ("far", 0), ("near", 5), ("spread", 3), ("near", 1), ("near", 6), ("pass_on", 0),
+    ("swap1", 5), ("far", 6), ("swap1", 4), ("spread", 2), ("far", 3), ("swap2", 6),
+    ("near", 3), ("share", 0), ("pass_on", 6), ("spread", 7), ("compute", 0), ("pass_on", 3),
+    ("far", 2), ("near", 2), ("far", 1), ("share", 3), ("swap0", 6), ("pass_on", 2),
+    ("far", 7), ("compute", 3), ("swap3", 6), ("pass_on", 1), ("share", 2), ("near", 7),
+    ("swap1", 6), ("far", 4), ("swap0", 4), ("pass_on", 7), ("far", 5), ("join", 0),
+    ("swap0", 5), ("join", 3), ("share", 1), ("swap0", 7), ("swap2", 7), ("pass_on", 5),
+    ("swap1", 7), ("side", 3), ("hop", 0), ("compute", 2), ("share", 7), ("pass_on", 4),
+    ("swap3", 7), ("compute", 1), ("hop", 3), ("side", 0), ("swap3", 5), ("join", 2),
+    ("share", 6), ("middle", 0), ("swap2", 4), ("compute", 7), ("hop", 2), ("swap2", 5),
+    ("join", 1), ("swap3", 4), ("hop", 1), ("middle", 3), ("join", 7), ("share", 4),
+    ("side", 1), ("side", 2), ("compute", 6), ("middle", 2), ("share", 5), ("finish", 3),
+    ("join", 6), ("hop", 6), ("side", 6), ("compute", 4), ("hop", 7), ("middle", 6),
+    ("finish", 2), ("join", 4), ("finish", 0), ("compute", 5), ("side", 7), ("middle", 7),
+    ("join", 5), ("hop", 5), ("middle", 1), ("finish", 6), ("side", 5), ("hop", 4),
+    ("middle", 5), ("finish", 7), ("side", 4), ("finish", 1), ("middle", 4), ("finish", 5),
     ("finish", 4),
 ]
 
@@ -371,12 +372,14 @@
         self.started = True
 
     def wait_send(self):
-        if self.started and not self.sent:
+        assert self.started
+        if not self.sent:
             self.copy.wait_send()
         self.sent = True
 
     def wait_recv(self):
-        if self.started and not self.landed:
+        assert self.started
+        if not self.landed:
             self.copy.wait_recv()
         self.landed = True
 
@@ -391,15 +394,16 @@
     return 1 - value if by else value
 
 
-def prepare_kernel(groups, private, shared, table_ref, tokens_ref, lists_ref, pick_ref, weight_ref):
+def route(groups, private, shared, routes_ref, scores_ref, tokens_ref, lists_ref, pick_ref, weight_ref):
     node = lax.axis_index("node")
     local = lax.axis_index("local")
     side, core, half = node // CORES, node % CORES, local // SHARDS
-    count = table_ref.shape[1]
+    count = tokens_ref.shape[0]
     listed = count // 2
     swap = shared // 2
-    first, second = table_ref[0:1, :], table_ref[1:2, :]
-    score_first, score_second = table_ref[2:3, :], table_ref[3:4, :]
+    names = routes_ref[...].astype(jnp.float32)
+    first, second = names[0:1], names[1:2]
+    score_first, score_second = scores_ref[0:1, :], scores_ref[1:2, :]
     total = score_first + score_second
     weight_first = (SCALE * score_first / total).astype(jnp.bfloat16).astype(jnp.float32)
     weight_second = (SCALE * score_second / total).astype(jnp.bfloat16).astype(jnp.float32)
@@ -458,7 +462,8 @@
             for dc in range(2):
                 weight_ref[r, dc] = jnp.broadcast_to(values[dc : dc + 1], (8, 128))
     pick = jnp.concatenate(picks, axis=0).astype(jnp.bfloat16)
-    pick_ref[...] = pick
+    for r in range(SQUARES):
+        pick_ref[r] = pick[r * listed : (r + 1) * listed]
     width = 1024
 
     def fill(step, carry):
@@ -471,25 +476,9 @@
     lax.fori_loop(0, tokens_ref.shape[1] // width, fill, 0)
 
 
-def prepare(table, tokens, groups, private, shared):
-    count, model_width = tokens.shape
-    vmem = pl.BlockSpec(memory_space=pltpu.VMEM)
-    return pl.pallas_call(
-        functools.partial(prepare_kernel, groups, private, shared),
-        out_shape=[
-            jax.ShapeDtypeStruct((SQUARES, count // 2, model_width), jnp.bfloat16),
-            jax.ShapeDtypeStruct((2 * count, count), jnp.bfloat16),
-            jax.ShapeDtypeStruct((SQUARES, CORES, 8, 128), jnp.float32),
-        ],
-        in_specs=[vmem, vmem],
-        out_specs=[vmem] * 3,
-        name="prepare",
-    )(table, tokens)
-
-
 def layer_kernel(
-    listed, swap, lists, weight, gate_hbm, up_hbm, down_hbm, ret,
-    gate, up, down, rows_a, rows_b, table, given_a, given_b, extra, held_a, held_b, hidden,
+    groups, private, shared_slots, tokens, routes, scores, gate_hbm, up_hbm, down_hbm, combined,
+    lists, pick, weight, ret, total, gate, up, down, rows_a, rows_b, table, given_a, given_b, extra, held_a, held_b, hidden,
     load_sem, own_sem, t_send, t_recv, send, recv,
 ):
     node = lax.axis_index("node")
@@ -497,6 +486,7 @@
     side, core = node // CORES, node % CORES
     half, block = local // SHARDS, local % SHARDS
     deep, across = block // 2, block % 2
+    listed, swap = lists.shape[1], shared_slots // 2
     part = listed // PARTS
     rows, given, held = (rows_a, rows_b), (given_a, given_b), (held_a, held_b)
     lane = [rows[p].shape[2] for p in range(PARTS)]
@@ -521,9 +511,12 @@
         for p in range(PARTS)
     ]
     own.append(pltpu.make_async_copy(weight.at[0, 0], table.at[0, 0, 0], own_sem.at[PARTS]))
-    for copy in own + loads:
+    for load in loads:
+        load.start()
+    route(groups, private, shared_slots, routes, scores, tokens, lists, pick, weight)
+    pl.semaphore_wait(barrier, len(offsets))
+    for copy in own:
         copy.start()
-    pl.semaphore_wait(barrier, len(offsets))
     waited = set()
 
     def once(*names):
@@ -734,6 +727,27 @@
             value = value + held[p][0, r].astype(jnp.float32) + held[p][1, r].astype(jnp.float32)
             piece(ret, 0, p)[...] = value.astype(ret.dtype)
 
+    def add_up(chunks, ending):
+        for q in chunks:
+            if q % SQUARES:
+                home[q].wait_recv()
+        wide = 1024
+        picked = jnp.concatenate([piece(pick, q % SQUARES, q // SQUARES)[...] for q in chunks], axis=0)
+
+        def step(k, carry):
+            columns = pl.ds(pl.multiple_of(k * wide, wide), wide)
+            back = jnp.concatenate(
+                [ret[q % SQUARES, pl.ds(q // SQUARES * part, part), columns] for q in chunks], axis=0
+            )
+            value = lax.dot_general(picked, back, (((0,), (0,)), ((), ())), preferred_element_type=jnp.float32)
+            if ending:
+                combined[:, columns] = (total[:, columns] + value).astype(combined.dtype)
+            else:
+                total[:, columns] = value
+            return carry
+
+        lax.fori_loop(0, ret.shape[2] // wide, step, 0)
+
     steps = dict(
         spread=lambda q: spread[q].start(), near=send_near, far=send_far, pass_on=pass_on, share=share,
         compute=compute, join=join, hop=send_hop, side=send_side, middle=middle, finish=finish,
@@ -743,14 +757,18 @@
         steps[f"swap{db}"] = functools.partial(swap_rows, db=db)
     for name, q in SCHEDULE:
         steps[name](q)
+    last = [q for name, q in SCHEDULE if name == "finish"]
+    add_up(last[:-LATE], False)
+    add_up(last[-LATE:], True)
     once(*range(PARTS + 4))
     for made in everything:
         made.wait_recv()
         made.wait_send()
 
 
-def layer(lists, weight, gate_proj, up_proj, down_proj, swap):
-    _, listed, model_width = lists.shape
+def layer(tokens, routes, scores, gate_proj, up_proj, down_proj, groups, private, shared):
+    count, model_width = tokens.shape
+    listed, swap = count // 2, shared // 2
     hidden_width = gate_proj.shape[2]
     part = listed // PARTS
     lanes = (SHARDS * part, SHARDS * (part + swap))
@@ -762,11 +780,16 @@
         return pltpu.VMEM(shape, jnp.bfloat16)
 
     return pl.pallas_call(
-        functools.partial(layer_kernel, listed, swap),
-        out_shape=jax.ShapeDtypeStruct(lists.shape, jnp.bfloat16),
-        in_specs=[vmem, vmem, hbm, hbm, hbm],
+        functools.partial(layer_kernel, groups, private, shared),
+        out_shape=jax.ShapeDtypeStruct(tokens.shape, tokens.dtype),
+        in_specs=[vmem, vmem, vmem, hbm, hbm, hbm],
         out_specs=vmem,
         scratch_shapes=[
+            space(SQUARES, listed, model_width),
+            space(SQUARES, listed, count),
+            pltpu.VMEM((SQUARES, CORES, 8, 128), jnp.float32),
+            space(SQUARES, listed, model_width),
+            pltpu.VMEM((count, model_width), jnp.float32),
             space(*gate_proj.shape[1:]),
             space(*up_proj.shape[1:]),
             space(*down_proj.shape[1:]),
@@ -790,7 +813,7 @@
             collective_id=2, has_side_effects=True, vmem_limit_bytes=67043328
         ),
         name="layer",
-    )(lists, weight, gate_proj, up_proj, down_proj)
+    )(tokens, routes, scores, gate_proj, up_proj, down_proj)
 
 
 def per_device(tokens, routes, scores, gate_proj, up_proj, down_proj):
@@ -804,12 +827,7 @@
     fits = private > 0 and shared > 0 and private % 8 == 0 and shared % 16 == 0 and token_count % 32 == 0
     if not (square and fits):
         return bucketed(tokens, routes, scores, gate_proj, up_proj, down_proj)
-    table = jnp.concatenate([routes.astype(jnp.float32), scores], axis=1).T
-    lists, pick, weight = prepare(table, tokens, groups, private, shared)
-    returned = layer(lists, weight, gate_proj, up_proj, down_proj, shared // 2)
-    flat = returned.reshape(-1, returned.shape[-1])
-    combined = lax.dot_general(pick, flat, (((0,), (0,)), ((), ())), preferred_element_type=jnp.float32)
-    return combined.astype(jnp.bfloat16)
+    return layer(tokens, routes.T, scores.T, gate_proj, up_proj, down_proj, groups, private, shared)
 
 
 def solution(mesh):

time: 177 us -> 166 us (0.938)
  Pallas kernels: 172 us -> 163 us
  matrix products: 2.88 us -> 0 us
  local copies, waits for them, and re-layouts: 0 us -> 2.16 us
  other arithmetic: 1.95 us -> 0 us
    pallas_call x2 -> x1, Pallas kernels: 172 us -> 163 us  [layer(): pl.pallas_call(functools.partial(layer_kernel, groups, private, shared),...]
    dot_general x1 -> x0, matrix products: 2.88 us -> none  [per_device(): lax.dot_general(pick, flat, (((0,), (0,)), ((), ())), preferred_element_t...]
    unnamed x0 -> x1, local copies, waits for them, and re-layouts: none -> 2.16 us
where the time goes in v2:
time: 166 us; the launch traced here: 165 us
  Pallas kernels  163 us (98%)
  local copies, waits for them, and re-layouts  2.16 us (1%)
    pallas_call x1, Pallas kernels, layer(): pl.pallas_call(functools.partial(layer_kernel, groups, private, shared),...  163 us

profile of v2, /device:TPU:0, one launch (start us, length us, event | category | flops | bytes accessed | tf_op | source)
XLA Modules:
  0.0 165.4 jit_solution(12302647552689628162)
XLA Ops:
  0.0 163.2 %layer.1 = bf16[64,7168]{1,0:T(8,128)(2,1)} custom-call(bf16[64,7168]{1,0:T(8,128)(2,1)} %tokens.1, s32[2,64]{1,0:T(2,128)} %bitcast.2, f32[2,64]{1,0:T(2,128)} %bitcast.3, bf16[1,7168,512]{2,1,0:T(8,128)(2,1)} %gate_hbm.1, bf16[1,7168,512]{2,1,0:T(8,128)(2,1)} %up_hbm.1, bf16[1,512,7168]{2,1,0:T(8,128)(2,1)} %down_hbm.1), custom_call_target="tpu_custom_call" | custom-call | tf_op jit(solution)/shard_map/layer/pallas_call | solution.py:782
  163.2 2.2 %copy.8 = bf16[64,7168]{1,0:T(8,128)(2,1)} copy(bf16[64,7168]{1,0:T(8,128)(2,1)} %layer.1) | data formatting | bytes 1835008
